TPU v7x, 32 devices: a whole 2x2x4 slice. The times are simulated.
32 devices in a mesh: seq: 8 (over z, x), dp: 4 (over y, core).
Axes of the slice: x: 2, y: 2, z: 4, core: 2. Of those that a mesh axis runs over, the one named last changes fastest.
Arguments:
- layer_input: bfloat16 [4096, 2560], P(('dp', 'seq')), may hold values from -6 to 6
- ssm_input: bfloat16 [4096, 2560], P(('dp', 'seq')), may hold values from -6 to 6
- out_grad: bfloat16 [4096, 2560], P(('dp', 'seq')), may hold values from -6 to 6
- b_weight: bfloat16 [2560, 128], replicated, may hold values from -0.125 to 0.125
- c_weight: bfloat16 [2560, 128], replicated, may hold values from -0.125 to 0.125
- dt_weight: bfloat16 [2560, 40], replicated, may hold values from -0.25 to 0.25
- dt_bias: float32 [40], replicated, may hold values from -9.7 to -8.2
- a_log: float32 [40], replicated, may hold values from -13 to 4.7
- d_skip: float32 [40], replicated, may hold values from 0.5 to 1.5
Outputs:
- grad_ssm_input: bfloat16 [4096, 2560], P(('dp', 'seq'))
- grad_layer_input: bfloat16 [4096, 2560], P(('dp', 'seq'))
- grad_b_weight: float32 [2560, 128], P('seq')
- grad_c_weight: float32 [2560, 128], P('seq')
- grad_dt_weight: float32 [2560, 40], P('seq')
- grad_dt_bias: float32 [40], replicated
- grad_a_log: float32 [40], replicated
- grad_d_skip: float32 [40], replicated
All inputs are finite; a program needn't handle non-finite values.
Results may differ from a plain program's by a relative error of at most 0.0018.
Values sent between devices are 32-bit elements; how exact they have to be, the bound alone decides.
No kernel may reach another device: no remote copies, remote signals or barrier semaphores. Data moves between devices by JAX's collectives and lax.ppermute only.
A program may use at most 256 MiB of HBM per device.

v0:
```python
import jax
import jax.numpy as jnp
from jax import lax
from jax.sharding import PartitionSpec as P

EXACT = lax.Precision.HIGHEST


def carried_in(value, axis, join, neutral, backward):
    count, mine = (lax.axis_size(axis), lax.axis_index(axis))
    pieces = jax.tree.map(lambda part: lax.all_gather(part, axis), value)
    if backward:
        pieces = jax.tree.map(lambda part: part[::-1], pieces)
        mine = count - 1 - mine
    running = jax.tree.map(
        lambda part, zero: jnp.full_like(part, 0) + jnp.asarray(zero, part.dtype), value, neutral
    )

    def step(position, running):
        longer = join(running, jax.tree.map(lambda part: part[position], pieces))
        return jax.tree.map(lambda new, old: jnp.where(position < mine, new, old), longer, running)

    return lax.fori_loop(0, count - 1, step, running)


def forward_combine(earlier, later):
    return (earlier[0] + later[0], jnp.exp(later[0])[:, None, None] * earlier[1] + later[1])


def reverse_combine(earlier, later):
    return (earlier[0] + later[0], later[1] + jnp.exp(later[0])[:, None, None] * earlier[1])


def body(layer_input, ssm_input, out_grad, b_weight, c_weight, dt_weight, dt_bias, a_log, d_skip):
    length = layer_input.shape[0]
    head_count = dt_bias.shape[0]
    state_size = b_weight.shape[1]
    head_width = ssm_input.shape[1] // head_count
    proj_b = jnp.dot(layer_input, b_weight, preferred_element_type=jnp.float32)
    proj_c = jnp.dot(layer_input, c_weight, preferred_element_type=jnp.float32)
    raw_dt = jnp.dot(layer_input, dt_weight, preferred_element_type=jnp.float32) + dt_bias[None, :]
    dt_values = jax.nn.softplus(raw_dt)
    decay_rate = -jnp.exp(a_log)
    log_decay = dt_values * decay_rate[None, :]
    row_index = lax.broadcasted_iota(jnp.int32, (length, length), 0)
    col_index = lax.broadcasted_iota(jnp.int32, (length, length), 1)
    causal = row_index >= col_index
    triangle = causal.astype(jnp.float32)
    cumulative = jnp.dot(triangle, log_decay, precision=EXACT)
    block_decay = cumulative[-1]
    to_end = jnp.exp(block_decay[None, :] - cumulative)
    from_start = jnp.exp(cumulative)
    inputs = ssm_input.astype(jnp.float32).reshape(length, head_count, head_width)
    cotangent = out_grad.astype(jnp.float32).reshape(length, head_count, head_width)
    scaled_inputs = (to_end * dt_values)[:, :, None] * inputs
    scaled_cotangent = from_start[:, :, None] * cotangent
    local_state = jnp.einsum("shp,sn->hpn", scaled_inputs, proj_b, precision=EXACT)
    local_back = jnp.einsum("thp,tn->hpn", scaled_cotangent, proj_c, precision=EXACT)
    identity = (
        jnp.zeros((head_count,), jnp.float32),
        jnp.zeros((head_count, head_width, state_size), jnp.float32),
    )
    carry_in = carried_in((block_decay, local_state), "seq", forward_combine, identity, False)[1]
    carry_out = carried_in((block_decay, local_back), "seq", reverse_combine, identity, True)[1]
    spread = cumulative.T[:, :, None] - cumulative.T[:, None, :]
    decay_table = jnp.exp(jnp.where(causal[None], spread, -1e30))
    scores = jnp.dot(proj_c, proj_b.T, precision=EXACT)
    pair_dots = jnp.einsum("thp,shp->hts", cotangent, inputs, precision=EXACT)
    weight = decay_table * scores[None]
    back_in = jnp.einsum("hst,shp->thp", weight, cotangent, precision=EXACT)
    back_carry = jnp.einsum("hpn,tn->thp", carry_out, proj_b, precision=EXACT)
    back_in = back_in + to_end[:, :, None] * back_carry
    grad_x = dt_values[:, :, None] * back_in + d_skip[None, :, None] * cotangent
    mixed_pairs = decay_table * pair_dots
    pair_sum = jnp.einsum("hts,sh->ts", mixed_pairs, dt_values, precision=EXACT)
    grad_b = jnp.dot(pair_sum.T, proj_c, precision=EXACT)
    grad_b = grad_b + jnp.einsum("thp,hpn->tn", scaled_inputs, carry_out, precision=EXACT)
    grad_c = jnp.dot(pair_sum, proj_b, precision=EXACT)
    grad_c = grad_c + jnp.einsum("thp,hpn->tn", scaled_cotangent, carry_in, precision=EXACT)
    pair_terms = weight * pair_dots * dt_values.T[:, None, :]
    front_carry = jnp.einsum("hpn,tn->thp", carry_in, proj_c, precision=EXACT)
    own_in = from_start * jnp.sum(cotangent * front_carry, axis=2)
    own_out = to_end * dt_values * jnp.sum(inputs * back_carry, axis=2)
    cross_term = jnp.exp(block_decay) * jnp.sum(carry_out * carry_in, axis=(1, 2))
    last_row = (lax.broadcasted_iota(jnp.int32, (length, 1), 0) == length - 1).astype(jnp.float32)
    change = jnp.sum(pair_terms, axis=2).T - jnp.sum(pair_terms, axis=1).T + own_in - own_out
    change = change + last_row * (cross_term + jnp.sum(own_out, axis=0))[None, :]
    grad_log = jnp.dot(triangle.T, change, precision=EXACT)
    direct = jnp.sum(inputs * back_in, axis=2)
    grad_raw = (direct + grad_log * decay_rate[None, :]) * jax.nn.sigmoid(raw_dt)
    grad_bias = jnp.sum(grad_raw, axis=0)
    grad_alog = jnp.sum(grad_log * dt_values, axis=0) * decay_rate
    grad_skip = jnp.sum(cotangent * inputs, axis=(0, 2))
    extras = jnp.stack([grad_bias, grad_alog, grad_skip])
    grad_cols = jnp.concatenate([grad_b, grad_c, grad_raw], axis=1)
    weights_wide = jnp.concatenate([b_weight, c_weight, dt_weight], axis=1).astype(jnp.float32)
    grad_u = jnp.dot(grad_cols, weights_wide.T, precision=EXACT).astype(jnp.bfloat16)
    u_wide = layer_input.astype(jnp.float32)
    row_grads = lax.psum_scatter(
        jnp.einsum("td,tk->dk", u_wide, grad_cols, precision=EXACT),
        "seq",
        scatter_dimension=0,
        tiled=True,
    )
    row_grads = lax.psum(row_grads, "dp")
    small_grads = lax.psum(extras, ("seq", "dp"))
    grad_x_out = grad_x.reshape(length, head_count * head_width).astype(jnp.bfloat16)
    return (
        grad_x_out,
        grad_u,
        row_grads[:, :state_size],
        row_grads[:, state_size : 2 * state_size],
        row_grads[:, 2 * state_size :],
        small_grads[0],
        small_grads[1],
        small_grads[2],
    )


def solution(mesh):
    in_specs = (
        P(("dp", "seq"), None),
        P(("dp", "seq"), None),
        P(("dp", "seq"), None),
        P(),
        P(),
        P(),
        P(),
        P(),
        P(),
    )
    out_specs = (
        P(("dp", "seq"), None),
        P(("dp", "seq"), None),
        P("seq", None),
        P("seq", None),
        P("seq", None),
        P(),
        P(),
        P(),
    )
    return jax.shard_map(body, mesh=mesh, in_specs=in_specs, out_specs=out_specs, check_vma=False)
```

profile of v0, /device:TPU:0, one launch (start us, length us, event | category | flops | bytes accessed | tf_op | source)
XLA Modules:
  0.0 509.1 jit_solution(5627975017452469384)
XLA Ops:
  11.0 2.2 fusion.30
  13.3 2.2 copy.58
  15.5 22.5 %all-gather.2 = f32[8,1,40]{2,1,0:T(1,128)S(1)} all-gather(f32[1,1,40]{2,1,0:T(1,128)S(1)} %bitcast.138), channel_id=1, replica_groups=mesh['seq'=8,'dp'=4] {'seq'}, dimensions={0}, use_global_device_ids=true | all-gather | bytes 1440 | tf_op jit(solution)/shard_map/all_gather | solution.py:11
  38.0 2.4 copy.62
  42.8 123.8 %all-gather.6.cloned.1.call-done = f32[320,64,128]{2,1,0:T(8,128)} async-done(((f32[40,64,128]{2,1,0:T(8,128)}), f32[320,64,128]{2,1,0:T(8,128)}) %all-gather.6.cloned.1.call-update) | async-done | bytes 10485776 | tf_op jit(solution)/shard_map/all_gather | solution.py:11
  166.6 10.0 %rev.6 = f32[8,40,64,128]{3,2,1,0:T(8,128)} reverse(f32[8,40,64,128]{3,2,1,0:T(8,128)} %bitcast.126), dimensions={0} | reverse | bytes 20971520 | tf_op jit(solution)/shard_map/rev | solution.py:13
  176.6 11.6 %while.28 = (s32[]{:T(128)}, f32[40,64,128]{2,1,0:T(8,128)S(1)}, s32[]{:T(128)}, f32[8,40,64,128]{3,2,1,0:T(8,128)}, f32[8,40]{1,0:T(8,128)S(1)}, /*index=5*/s32[]{:T(128)}, s32[]{:T(128)}) while((s32[]{:T(128)}, f32[40,64,128]{2,1,0:T(8,128)S(1)}, s32[]{:T(128)}, f32[8,40,64,128]{3,2,1,0:T(8,128)}, f32[8,40]{1,0:T(8,128)S(1)}, ...), condition=%wide.region_1.2_spmd.clone, body=%wide.region_0.1_spmd.clone.sunk | while | flops 1310724 | bytes 3932745 | solution.py:23
  176.6 1.6 fusion.99
  178.3 1.6 fusion.99
  179.9 1.6 fusion.99
  181.6 1.6 fusion.99
  183.2 1.6 fusion.99
  184.9 1.6 fusion.99
  186.6 1.6 fusion.99
  189.7 3.8 multiply_reduce_fusion.3
  194.2 2.2 fusion.24
  196.7 2.2 copy.61
  199.4 3.9 fusion.10
  203.3 1.8 multiply_reduce_fusion
  205.1 2.2 fusion.35
  208.3 137.0 %all-gather.8.cloned.1.call-done = f32[320,64,128]{2,1,0:T(8,128)} async-done(((f32[40,64,128]{2,1,0:T(8,128)}), f32[320,64,128]{2,1,0:T(8,128)}) %all-gather.8.cloned.1.call-update) | async-done | bytes 10485776 | tf_op jit(solution)/shard_map/all_gather | solution.py:11
  345.3 19.9 %while.29 = (s32[]{:T(128)}, f32[40,64,128]{2,1,0:T(8,128)S(1)}, s32[]{:T(128)}, f32[8,40]{1,0:T(8,128)}, f32[8,40,64,128]{3,2,1,0:T(8,128)}, /*index=5*/s32[]{:T(128)}, s32[]{:T(128)}) while((s32[]{:T(128)}, f32[40,64,128]{2,1,0:T(8,128)S(1)}, s32[]{:T(128)}, f32[8,40]{1,0:T(8,128)}, f32[8,40,64,128]{3,2,1,0:T(8,128)}, ...), condition=%wide.region_3.4_spmd.clone, body=%wide.region_2.3_spmd.clone.sunk | while | flops 1310724 | bytes 3932745 | solution.py:23
  349.3 1.6 fusion.100
  367.8 2.3 fusion.32
  370.8 3.0 convolution_bitcast_fusion
  373.8 5.0 copy.74
  381.2 2.4 copy.64
  383.6 41.1 %psum.15 = f32[3,40]{1,0:T(4,128)S(1)} all-reduce(f32[3,40]{1,0:T(4,128)S(1)} %pad_maximum_fusion.3), channel_id=1, replica_groups=mesh['seq'=8,'dp'=4] {'seq','dp'}, use_global_device_ids=true, to_apply=%region_17.18 | all-reduce | flops 120 | bytes 960 | tf_op jit(solution)/shard_map/psum | solution.py:106
  424.8 3.0 convolution_convert_fusion
  427.8 35.8 %reduce-scatter.4.cloned.1.call-done = f32[320,296]{1,0:T(8,128)} async-done(((f32[2560,296]{1,0:T(8,128)}), f32[320,296]{1,0:T(8,128)}) %reduce-scatter.4.cloned.1.call-update) | async-done | bytes 378896
  463.6 2.0 copy.75
  466.2 32.3 %all-reduce.2.cloned.1.call-done = f32[320,296]{0,1:T(8,128)} async-done(((f32[320,296]{0,1:T(8,128)}), f32[320,296]{0,1:T(8,128)}) %all-reduce.2.cloned.1.call-update) | async-done | bytes 378896 | tf_op jit(solution)/shard_map/psum | solution.py:105
  (133 shorter events, 38.3 us)
Async XLA Ops:
  7.2 2.9 copy-start.6
  7.2 159.4 %all-gather.6.cloned.1.call-start = ((), (), s32[]{:S(2)}) async-start(), calls=%async_computation.2 | async-start | bytes 11796480 | tf_op jit(solution)/shard_map/all_gather | solution.py:11
  9.6 179.9 %copy-start.17 = (f32[128,40]{0,1:T(8,128)}, f32[128,40]{0,1:T(8,128)S(1)}, u32[]{:S(2)}) copy-start(f32[128,40]{0,1:T(8,128)S(1)} %get-tuple-element.311) | copy-start | bytes 61444
  10.0 5.5 %copy-start.24 = (f32[1,40]{1,0:T(1,128)}, f32[1,40]{1,0:T(1,128)S(1)}, u32[]{:S(2)}) copy-start(f32[1,40]{1,0:T(1,128)S(1)} %copy.76) | copy-start | bytes 484
  10.7 178.8 %copy-start.1 = (f32[128,2560]{0,1:T(8,128)}, f32[128,2560]{0,1:T(8,128)S(1)}, u32[]{:S(2)}) copy-start(f32[128,2560]{0,1:T(8,128)S(1)} %copy.60) | copy-start | bytes 3932164
  13.3 332.0 %all-gather.8.cloned.1.call-start = ((), (), s32[]{:S(2)}) async-start(), calls=%async_computation.3 | async-start | bytes 11796480 | tf_op jit(solution)/shard_map/all_gather | solution.py:11
  38.0 2.4 copy-start.23
  40.5 158.9 %copy-start.19 = (pred[128,128]{1,0:T(8,128)(4,1)}, pred[128,128]{1,0:T(8,128)(4,1)S(1)}, u32[]{:S(2)}) copy-start(pred[128,128]{1,0:T(8,128)(4,1)S(1)} %iota_compare_fusion) | copy-start | bytes 49156
  188.2 1.5 copy-start.12
  188.2 1.5 copy-start.20
  193.5 2.9 copy-start.21
  196.4 267.2 %reduce-scatter.4.cloned.1.call-start = ((), (), s32[]{:S(2)}) async-start(), calls=%async_computation.4 | async-start | bytes 4423680
  199.4 3.9 copy-start.18
  203.3 1.8 copy-start.4
  367.7 2.7 copy-start.25
  367.8 2.7 copy-start.26
  367.8 2.7 copy-start.22
  367.8 2.7 copy-start.30
  367.8 2.7 copy-start.31
  367.8 2.7 copy-start.32
  367.8 2.7 copy-start.33
  367.8 2.7 copy-start.34
  367.8 3.0 copy-start.14
  370.4 3.4 copy-start.15
  378.8 2.0 copy-start.5
  378.8 2.0 copy-start.7
  378.8 119.7 %all-reduce.2.cloned.1.call-start = ((), (), s32[]{:S(2)}) async-start(), calls=%async_computation.1 | async-start | bytes 909312 | tf_op jit(solution)/shard_map/psum | solution.py:105
  380.8 2.8 copy-start.28
  380.8 44.0 %copy-start.10 = (bf16[2560,128]{1,0:T(8,128)(2,1)S(1)}, bf16[2560,128]{1,0:T(8,128)(2,1)}, u32[]{:S(2)}) copy-start(bf16[2560,128]{1,0:T(8,128)(2,1)} %param.17) | copy-start | bytes 1966084
  380.8 43.9 %copy-start.11 = (bf16[2560,128]{1,0:T(8,128)(2,1)S(1)}, bf16[2560,128]{1,0:T(8,128)(2,1)}, u32[]{:S(2)}) copy-start(bf16[2560,128]{1,0:T(8,128)(2,1)} %param.16) | copy-start | bytes 1966084
  380.8 43.9 %copy-start.16 = (f32[128,128]{0,1:T(8,128)S(1)}, f32[128,128]{0,1:T(8,128)}, u32[]{:S(2)}) copy-start(f32[128,128]{0,1:T(8,128)} %copy-done.15) | copy-start | bytes 196612
  381.0 43.7 %copy-start.13 = (bf16[2560,40]{1,0:T(8,128)(2,1)S(1)}, bf16[2560,40]{1,0:T(8,128)(2,1)}, u32[]{:S(2)}) copy-start(bf16[2560,40]{1,0:T(8,128)(2,1)} %copy.63) | copy-start | bytes 614404
  (7 other events, 8.5 us)
Sparse Core Ops, SparseCore 0:
  13.4 153.1 all-gather.5
  196.6 148.6 all-gather.7
  378.9 84.6 reduce-scatter.3
  465.8 32.6 all-reduce.1
where the time goes:
time: 511 us; the launch traced here: 509 us
  waiting for transfers between devices  329 us (64%)
  blocking collectives  63.7 us (12%)
  local copies, waits for them, and re-layouts  43.2 us (8%)
  matrix products  30.9 us (6%)
  other arithmetic  27.2 us (5%)
  between operations  14.3 us (3%)
    all_gather x2, waiting for transfers between devices, carried_in(): pieces = jax.tree.map(lambda part: lax.all_gather(part, axis), value)  261 us
    psum x1, blocking collectives, body(): small_grads = lax.psum(extras, ('seq', 'dp'))  41.1 us
    unnamed x5, waiting for transfers between devices  35.9 us
    psum x1, waiting for transfers between devices, body(): row_grads = lax.psum(row_grads, 'dp')  32.3 us
    select_n x14, other arithmetic, step(): jnp.where(position < mine, new, old)  22.6 us
    all_gather x1, blocking collectives, carried_in(): pieces = jax.tree.map(lambda part: lax.all_gather(part, axis), value)  22.5 us
    unnamed x79, local copies, waits for them, and re-layouts  18.9 us
  transfers between devices with their start and end apart: 4, of which 4 were waited for; matrix products, arithmetic and copies ran while one was open for 5% of the time, Pallas kernels for 0%

commit v1 on v0

v1 whole, which is shorter than its diff:
```python
import jax
import jax.numpy as jnp
from jax import lax
from jax.experimental import pallas as pl
from jax.experimental.pallas import tpu as pltpu
from jax.sharding import PartitionSpec as P

F32 = jnp.float32
BF16 = jnp.bfloat16
LANES = 128
CHUNKS = 2

NN = (((1,), (0,)), ((), ()))
NT = (((1,), (1,)), ((), ()))
TN = (((0,), (0,)), ((), ()))


def mm(a, b, dims):
    return lax.dot_general(a, b, dims, preferred_element_type=F32)


def split2(a):
    hi = a.astype(BF16)
    return hi, (a - hi.astype(F32)).astype(BF16)


def split3(a):
    hi = a.astype(BF16)
    rest = a - hi.astype(F32)
    mid = rest.astype(BF16)
    return hi, mid, (rest - mid.astype(F32)).astype(BF16)


def dot3(a, b, dims):
    ah, al = split2(a)
    bh, bl = split2(b)
    return mm(ah, bh, dims) + (mm(ah, bl, dims) + mm(al, bh, dims))


def dot_left(a, b, dims):
    ah, al = split2(a)
    return mm(ah, b, dims) + mm(al, b, dims)


def dot_left_full(a, b, dims):
    ah, am, al = split3(a)
    return mm(ah, b, dims) + (mm(am, b, dims) + mm(al, b, dims))


def dot_right_full(a, b, dims):
    bh, bm, bl = split3(b)
    return mm(a, bh, dims) + (mm(a, bm, dims) + mm(a, bl, dims))


def iota(shape, axis):
    return lax.broadcasted_iota(jnp.int32, shape, axis)


def log1p_unit(y):
    s = y / (2.0 + y)
    q = s * s
    poly = jnp.full_like(q, 1.0 / 17)
    for k in (15, 13, 11, 9, 7, 5, 3, 1):
        poly = poly * q + 1.0 / k
    return 2.0 * s * poly


def triangle(length, lower):
    r, c = iota((length, length), 0), iota((length, length), 1)
    keep = (r >= c) if lower else (c >= r)
    return jnp.where(keep, 1.0, 0.0).astype(BF16)


def expand_matrix(head_start, width, lanes):
    r, c = iota((LANES, lanes), 0), iota((LANES, lanes), 1)
    return jnp.where(r == head_start + c // width, 1.0, 0.0).astype(BF16)


def collect_matrix(head_start, width, lanes):
    r, c = iota((lanes, LANES), 0), iota((lanes, LANES), 1)
    return jnp.where(c == head_start + r // width, 1.0, 0.0).astype(BF16)


def coefficients(tile, heads_all, heads_half):
    lane = iota(tile.shape, 1) < heads_half
    length = tile.shape[0]
    dt = jnp.where(lane, tile, 0.0)
    cum = jnp.where(lane, pltpu.roll(tile, LANES - heads_all, 1), 0.0)
    last = cum[length - 1 : length, :]
    from_start = jnp.where(lane, jnp.exp(cum), 0.0)
    to_end = jnp.where(lane, jnp.exp(last - cum), 0.0)
    decay = jnp.where(lane[:1], jnp.exp(last), 0.0)
    return dt, cum, from_start, to_end, decay


def row_of(v, rows=8):
    return jnp.broadcast_to(v, (rows, v.shape[1]))


def proj_kernel(at_ref, u_ref, wb_ref, wc_ref, wd_ref, bias_ref, alog_ref, own_ref, snd_ref, *, heads):
    length = u_ref.shape[0]
    state = wb_ref.shape[1]
    u = u_ref[...]
    b = mm(u, wb_ref[...], NN)
    c = mm(u, wc_ref[...], NN)
    raw = mm(u, wd_ref[...], NN) + bias_ref[...]
    dt = jnp.maximum(raw, 0.0) + log1p_unit(jnp.exp(-jnp.abs(raw)))
    sig = 1.0 / (1.0 + jnp.exp(-raw))
    log_decay = dt * -jnp.exp(alog_ref[...])
    cum = dot_right_full(triangle(length, True), log_decay, NN)
    lane = iota(raw.shape, 1)
    tile = jnp.where(lane < heads, dt, jnp.where(lane < 2 * heads, cum, sig))
    half = heads // 2
    at = at_ref[0]
    own_ref[:, :state] = b
    own_ref[:, state : 2 * state] = c
    own_ref[:, 2 * state :] = pltpu.roll(tile, (LANES - half * at) % LANES, 1)
    snd_ref[:, :state] = b
    snd_ref[:, state : 2 * state] = c
    snd_ref[:, 2 * state :] = pltpu.roll(tile, (LANES - half * (1 - at)) % LANES, 1)


def state_kernel(
    at_ref, xo_ref, go_ref, xgr_ref, po_ref, pr_ref, p_ref, q_ref, sf_ref, gs_ref, d_ref, *, heads, width, start
):
    half = heads // 2
    state = (po_ref.shape[1] - LANES) // 2
    lanes = xo_ref.shape[1]
    spread = expand_matrix(start, width, lanes)
    first_is_own = at_ref[0] == 0

    def local(x, g, pack_ref):
        dt, cum, from_start, to_end, decay = coefficients(pack_ref[:, 2 * state :], heads, half)
        xw = x * dot_left(to_end * dt, spread, NN)
        gw = g * dot_left(from_start, spread, NN)
        s = dot3(pack_ref[:, :state], xw, TN)
        back = dot3(pack_ref[:, state : 2 * state], gw, TN)
        return s, back, dot_left_full(row_of(decay), spread, NN)

    s_own, b_own, d_own = local(xo_ref[...].astype(F32), go_ref[...].astype(F32), po_ref)
    s_rcv, b_rcv, d_rcv = local(xgr_ref[0], xgr_ref[1], pr_ref)

    def pick(a, b):
        return jnp.where(first_is_own, a, b)

    s_first, s_second = pick(s_own, s_rcv), pick(s_rcv, s_own)
    b_first, b_second = pick(b_own, b_rcv), pick(b_rcv, b_own)
    d_first, d_second = pick(d_own, d_rcv), pick(d_rcv, d_own)
    p_ref[...] = d_second[:1] * s_first + s_second
    q_ref[...] = d_first[:1] * b_second + b_first
    sf_ref[...] = s_first
    gs_ref[...] = b_second
    d_ref[...] = d_first * d_second


def intra_kernel(
    xo_ref, go_ref, *refs, heads, width, chunks
):
    xgr_refs = refs[:chunks]
    po_ref, pr_ref = refs[chunks : chunks + 2]
    back_ref, gbc_ref, rows_ref = refs[chunks + 2 : chunks + 5]
    x_ref, g_ref, cumt_ref, acc_ref = refs[chunks + 5 :]
    length, lanes = xo_ref.shape
    half = heads // 2
    state = (po_ref.shape[1] - LANES) // 2
    part = lanes // chunks
    x_ref[0] = xo_ref[...]
    g_ref[0] = go_ref[...]
    for j in range(chunks):
        x_ref[1, :, j * part : (j + 1) * part] = xgr_refs[j][0].astype(BF16)
        g_ref[1, :, j * part : (j + 1) * part] = xgr_refs[j][1].astype(BF16)
    src, dst = iota((length, length), 0), iota((length, length), 1)
    causal = dst >= src
    low = iota((length, LANES), 1) < width
    for which, pack_ref in ((0, po_ref), (1, pr_ref)):
        b = pack_ref[:, :state]
        c = pack_ref[:, state : 2 * state]
        tile = pack_ref[:, 2 * state :]
        scores = dot3(b, c, NT)
        cumt_ref[...] = jnp.transpose(pltpu.roll(tile, LANES - heads, 1))
        acc_ref[...] = jnp.zeros_like(acc_ref)

        def step(k, _):
            at = pl.multiple_of(k * LANES, LANES)
            xp = x_ref[which, :, pl.ds(at, LANES)]
            gp = g_ref[which, :, pl.ds(at, LANES)]
            zero = jnp.zeros_like(xp)
            x2 = jnp.concatenate([jnp.where(low, xp, zero), jnp.where(low, zero, xp)], axis=0)
            g2 = jnp.concatenate([jnp.where(low, gp, zero), jnp.where(low, zero, gp)], axis=0)
            dots = mm(x2, gp, NT)
            turned = pltpu.roll(tile, LANES - 2 * k, 1)
            his, los = [], []
            total = acc_ref[...]
            for e in range(2):
                h = 2 * k + e
                dt_col = jnp.broadcast_to(turned[:, e : e + 1], (length, length))
                cum_col = jnp.broadcast_to(turned[:, heads + e : heads + e + 1], (length, length))
                cum_row = cumt_ref[pl.ds(h, 1), :]
                table = jnp.exp(jnp.where(causal, cum_row - cum_col, -1e30))
                pairs = table * dots[e * length : (e + 1) * length] * dt_col
                total = total + pairs
                rows_ref[which, pl.ds(h, 1), :] = jnp.sum(pairs * scores, axis=0, keepdims=True)
                hi, lo = split2(table * scores)
                his.append(hi)
                los.append(lo)
            acc_ref[...] = total
            back = mm(jnp.concatenate(his, axis=1), g2, NN) + mm(jnp.concatenate(los, axis=1), g2, NN)
            back_ref[which, :, pl.ds(at, LANES)] = back
            return 0

        rows_ref[which] = jnp.zeros(rows_ref.shape[1:], F32)
        lax.fori_loop(0, lanes // LANES, step, 0)
        pair_sum = acc_ref[...]
        gbc_ref[which, :, :state] = dot3(pair_sum, c, NN)
        gbc_ref[which, :, state:] = dot3(pair_sum, b, TN)


def carry_kernel(
    at_ref, xo_ref, go_ref, *refs, heads, width, chunks
):
    xgr_refs = refs[:chunks]
    sf_refs = refs[chunks : 2 * chunks]
    gs_refs = refs[2 * chunks : 3 * chunks]
    ci_refs = refs[3 * chunks : 4 * chunks]
    co_refs = refs[4 * chunks : 5 * chunks]
    po_ref, pr_ref, back_ref, gbc_ref, rows_ref, skip_ref, rate_ref = refs[5 * chunks : 5 * chunks + 7]
    gxo_ref, gxs_ref, pko_ref, pks_ref, extra_ref = refs[5 * chunks + 7 :]
    length, all_lanes = xo_ref.shape
    half = heads // 2
    state = (po_ref.shape[1] - LANES) // 2
    lanes = all_lanes // chunks
    own_first = at_ref[0] == 0
    rate = rate_ref[...]
    packs = (po_ref, pr_ref)
    co = [coefficients(r[:, 2 * state :], heads, half) for r in packs]
    zeros = jnp.zeros((length, LANES), F32)
    gb, gc = [gbc_ref[w, :, :state] for w in (0, 1)], [gbc_ref[w, :, state:] for w in (0, 1)]
    r_intra, r_back, r_front = [zeros, zeros], [zeros, zeros], [zeros, zeros]
    cross = [jnp.zeros((8, LANES), F32) for _ in (0, 1)]
    skip_sum = jnp.zeros((8, LANES), F32)
    for j in range(chunks):
        start = j * (half // chunks)
        spread = expand_matrix(start, width, lanes)
        collect = collect_matrix(start, width, lanes)
        cols = slice(j * lanes, (j + 1) * lanes)
        decays = [dot_left_full(row_of(co[w][4]), spread, NN)[:1] for w in (0, 1)]
        cin, cout = ci_refs[j][...], co_refs[j][...]
        d_first = jnp.where(own_first, decays[0], decays[1])
        d_second = jnp.where(own_first, decays[1], decays[0])
        cin_second = d_first * cin + sf_refs[j][...]
        cout_first = d_second * cout + gs_refs[j][...]
        for w in (0, 1):
            is_first = own_first if w == 0 else jnp.logical_not(own_first)
            my_in = jnp.where(is_first, cin, cin_second)
            my_out = jnp.where(is_first, cout_first, cout)
            dt, cum, from_start, to_end, decay = co[w]
            if w == 0:
                x, g = xo_ref[:, cols].astype(F32), go_ref[:, cols].astype(F32)
            else:
                x, g = xgr_refs[j][0], xgr_refs[j][1]
            b, c = packs[w][:, :state], packs[w][:, state : 2 * state]
            front = dot3(c, my_in, NN)
            back = dot3(b, my_out, NN)
            dt_wide = dot_left(dt, spread, NN)
            te_wide = dot_left(to_end, spread, NN)
            fs_wide = dot_left(from_start, spread, NN)
            intra = back_ref[w, :, cols]
            grad_x = dt_wide * (intra + te_wide * back) + skip_ref[:1, cols] * g
            if w == 0:
                gxo_ref[:, cols] = grad_x.astype(BF16)
            else:
                gxs_ref[:, cols] = grad_x
            r_intra[w] = r_intra[w] + dot_left_full(x * intra, collect, NN)
            r_back[w] = r_back[w] + dot_left_full(x * back, collect, NN)
            r_front[w] = r_front[w] + dot_left_full(g * front, collect, NN)
            gb[w] = gb[w] + dot3(x * (te_wide * dt_wide), my_out, NT)
            gc[w] = gc[w] + dot3(g * fs_wide, my_in, NT)
            both = jnp.sum(my_in * my_out, axis=0, keepdims=True)
            cross[w] = cross[w] + dot_left_full(row_of(both), collect, NN)
            skip_sum = skip_sum + dot_left_full(row_of(jnp.sum(x * g, axis=0, keepdims=True)), collect, NN)
    later = triangle(length, False)
    last_row = iota((length, LANES), 0) == length - 1
    bias_sum = jnp.zeros((1, LANES), F32)
    alog_sum = jnp.zeros((1, LANES), F32)
    lane = iota((length, LANES), 1) < half
    for w, out_ref in ((0, pko_ref), (1, pks_ref)):
        dt, cum, from_start, to_end, decay = co[w]
        sig = pltpu.roll(packs[w][:, 2 * state :], LANES - 2 * heads, 1)
        own_out = to_end * dt * r_back[w]
        change = jnp.transpose(rows_ref[w]) - dt * r_intra[w] + from_start * r_front[w] - own_out
        tail = decay * cross[w][:1] + jnp.sum(own_out, axis=0, keepdims=True)
        change = change + jnp.where(last_row, tail, 0.0)
        grad_log = dot_right_full(later, change, NN)
        direct = r_intra[w] + to_end * r_back[w]
        grad_raw = jnp.where(lane, (direct + grad_log * rate[:1]) * sig, 0.0)
        bias_sum = bias_sum + jnp.sum(grad_raw, axis=0, keepdims=True)
        alog_sum = alog_sum + jnp.sum(grad_log * dt, axis=0, keepdims=True) * rate[:1]
        out_ref[:, :state] = gb[w]
        out_ref[:, state : 2 * state] = gc[w]
        out_ref[:, 2 * state :] = grad_raw
    row = iota((8, LANES), 0)
    extra = jnp.where(row == 0, bias_sum, jnp.where(row == 1, alog_sum, jnp.where(row == 2, skip_sum[:1], 0.0)))
    extra_ref[...] = jnp.where(iota((8, LANES), 1) < half, extra, 0.0)


def join_kernel(at_ref, own_ref, rcv_ref, extra_ref, out_ref, extra_out_ref, *, heads):
    state = (own_ref.shape[1] - LANES) // 2
    half = heads // 2
    at = at_ref[0]
    out_ref[:, : 2 * state] = own_ref[:, : 2 * state] + rcv_ref[:, : 2 * state]
    mine = pltpu.roll(own_ref[:, 2 * state :], half * at, 1)
    other = pltpu.roll(rcv_ref[:, 2 * state :], half * (1 - at), 1)
    out_ref[:, 2 * state :] = mine + other
    extra_out_ref[...] = pltpu.roll(extra_ref[...], half * at, 1)


def merge_kernel(at_ref, own_ref, rcv_ref, out_ref):
    lanes = own_ref.shape[1]
    mine = pl.multiple_of(at_ref[0] * lanes, LANES)
    other = pl.multiple_of((1 - at_ref[0]) * lanes, LANES)
    out_ref[:, pl.ds(mine, lanes)] = own_ref[...]
    out_ref[:, pl.ds(other, lanes)] = rcv_ref[...].astype(BF16)


def grad_u_kernel(cols_ref, wb_ref, wc_ref, wd_ref, out_ref):
    state = wb_ref.shape[1]
    total = dot_left(cols_ref[:, :state], wb_ref[...], NT)
    total = total + dot_left(cols_ref[:, state : 2 * state], wc_ref[...], NT)
    total = total + dot_left(cols_ref[:, 2 * state :], wd_ref[...], NT)
    out_ref[...] = total.astype(BF16)


def weight_kernel(*refs, pieces, heads, state):
    u = jnp.concatenate([r[i].astype(BF16) for r in refs[:pieces] for i in range(r.shape[0])], axis=0)
    cols = jnp.concatenate([r[i] for r in refs[pieces : 2 * pieces] for i in range(r.shape[0])], axis=0)
    extra_ref, out_ref = refs[2 * pieces :]
    count, block, _ = out_ref.shape
    each = (block - heads) // 2
    hi, lo = split2(cols[:, : 2 * state])
    wide = mm(u, hi, TN) + mm(u, lo, TN)
    thi, tlo = split2(cols[:, 2 * state :])
    turned = mm(thi, u, TN) + mm(tlo, u, TN)
    turned = jnp.concatenate([turned[:heads], jnp.zeros((heads, LANES), F32)], axis=1)
    tail = jnp.transpose(jnp.concatenate([extra_ref[...], jnp.zeros((LANES - 8, LANES), F32)], axis=0))
    tail = pltpu.roll(tail, each, 1)[:heads]
    lane = iota((heads, LANES), 1)
    for s in range(count):
        rows = slice(s * each, (s + 1) * each)
        out_ref[s, :each] = wide[rows, :state]
        out_ref[s, each : 2 * each] = wide[rows, state:]
        start = s * each // LANES * LANES
        window = pltpu.roll(turned[:, start : start + 2 * LANES], (2 * LANES + start - s * each) % (2 * LANES), 1)
        out_ref[s, 2 * each :] = jnp.where(lane < each, window[:, :LANES], tail)


def final_kernel(at_ref, *refs, pieces, heads, order):
    parts = [r[i] for r in refs[:pieces] for i in range(r.shape[0])]
    gb_ref, gc_ref, gd_ref, bias_ref, alog_ref, skip_ref = refs[pieces:]
    each = gb_ref.shape[0] // len(parts)
    mine = at_ref[0]
    total = None
    for d in range(len(parts)):
        block = parts[0]
        for part, flip in list(zip(parts, order))[1:]:
            block = jnp.where(mine == d ^ flip, part, block)
        rows = slice(d * each, (d + 1) * each)
        gb_ref[rows] = block[:each]
        gc_ref[rows] = block[each : 2 * each]
        tail = jnp.concatenate([block[2 * each :], jnp.zeros((LANES - heads, LANES), F32)], axis=0)
        turned = jnp.transpose(tail)
        gd_ref[rows] = turned[:each, :heads]
        total = turned if total is None else total + turned
    bias_ref[...] = total[each : each + 1, :heads]
    alog_ref[...] = total[each + 1 : each + 2, :heads]
    skip_ref[...] = total[each + 2 : each + 3, :heads]


def vmem(n):
    return [pl.BlockSpec(memory_space=pltpu.VMEM) for _ in range(n)]


def call(kernel, n_in, outs, scratch=(), flops=10**8, scalar=True, name=None):
    specs = ([pl.BlockSpec(memory_space=pltpu.SMEM)] if scalar else []) + vmem(n_in)
    return pl.pallas_call(
        kernel,
        in_specs=specs,
        out_specs=vmem(len(outs)),
        out_shape=[jax.ShapeDtypeStruct(s, t) for s, t in outs],
        scratch_shapes=list(scratch),
        cost_estimate=pl.CostEstimate(flops=flops, transcendentals=0, bytes_accessed=10**6),
        compiler_params=pltpu.CompilerParams(vmem_limit_bytes=48 << 20),
        name=name,
    )


def body(layer_input, ssm_input, out_grad, b_weight, c_weight, dt_weight, dt_bias, a_log, d_skip):
    import functools

    length, model = layer_input.shape
    heads = dt_bias.shape[0]
    state = b_weight.shape[1]
    width = ssm_input.shape[1] // heads
    half = heads // 2
    lanes = half * width
    part = lanes // CHUNKS
    count = lax.axis_size("seq")
    place = lax.axis_index("seq") % 2
    at = jnp.reshape(place, (1,)).astype(jnp.int32)
    swap = [(i, i ^ 1) for i in range(count)]
    up = [(i, i + 2) for i in range(count - 2)]
    down = [(i + 2, i) for i in range(count - 2)]
    pack = 2 * state + LANES

    def exchange(value):
        return lax.ppermute(value, "seq", swap)

    def half_of(value, which, j=None):
        if j is None:
            return lax.dynamic_slice(value, (0, which * lanes), (length, lanes))
        return lax.dynamic_slice(value, (0, which * lanes + j * part), (length, part))

    groups = lax.axis_size("dp")
    group = lax.axis_index("dp")
    each = model // count // groups
    bits = []
    while groups >> (len(bits) + 1):
        bits.insert(0, 1 << len(bits))

    def spread_pieces(value):
        pieces = [value]
        for bit in bits:
            sent = pieces[0] if len(pieces) == 1 else jnp.concatenate(pieces, axis=0)
            pieces.append(lax.ppermute(sent, "dp", [(d, d ^ bit) for d in range(groups)]))
        return pieces

    def column_pieces(value):
        value = value.reshape(length, count, groups, each).transpose(2, 0, 1, 3)
        pieces = [value.reshape(groups, 1, length, count * each)]
        for bit in bits:
            high = (group // bit) % 2

            def side(piece, which):
                return lax.dynamic_slice_in_dim(piece, which * bit, bit, axis=0)

            sent = jnp.concatenate([side(p, 1 - high).astype(F32) for p in pieces], axis=1)
            pieces = [side(p, high) for p in pieces]
            pieces.append(lax.ppermute(sent, "dp", [(d, d ^ bit) for d in range(groups)]))
        return [p[0] for p in pieces]

    received = []
    for j in range(CHUNKS):
        both = jnp.stack([half_of(v, 1 - place, j).astype(F32) for v in (ssm_input, out_grad)])
        received.append(both)
    tripled = jnp.pad(jnp.concatenate([dt_weight] * 3, axis=1), ((0, 0), (0, LANES - 3 * heads)))

    def row3(v):
        return jnp.pad(jnp.concatenate([v] * 3), (0, LANES - 3 * heads))[None]

    own, send = call(
        functools.partial(proj_kernel, heads=heads), 6, [((length, pack), F32)] * 2, name="proj"
    )(at, layer_input, b_weight, c_weight, tripled, row3(dt_bias), row3(a_log))
    first = exchange(received[0])
    send, *rest = lax.optimization_barrier((send, *received[1:]))
    rcv = exchange(send)
    received = [first] + [exchange(v) for v in rest]
    u_pieces = column_pieces(layer_input)
    x_own, g_own = half_of(ssm_input, place), half_of(out_grad, place)

    carried, locals_ = [], []
    for j in range(CHUNKS):
        p, q, s_first, g_second, decay = call(
            functools.partial(
                state_kernel, heads=heads, width=width, start=j * (half // CHUNKS)
            ),
            5,
            [((state, part), F32)] * 4 + [((8, part), F32)],
            name="state",
        )(at, x_own[:, j * part : (j + 1) * part], g_own[:, j * part : (j + 1) * part], received[j], own, rcv)
        carried.append((p, q, decay[:1]))
        locals_.append((s_first, g_second))
    ins, outs = [], []
    for p, q, decay in carried:
        inward = lax.ppermute(p, "seq", up)
        outward = lax.ppermute(q, "seq", down)
        for _ in range(count // 2 - 2):
            inward = lax.ppermute(p + decay * inward, "seq", up)
            outward = lax.ppermute(q + decay * outward, "seq", down)
        ins.append(inward)
        outs.append(outward)
    back, grad_bc, rows = call(
        functools.partial(intra_kernel, heads=heads, width=width, chunks=CHUNKS),
        4 + CHUNKS,
        [((2, length, lanes), F32), ((2, length, 2 * state), F32), ((2, LANES, length), F32)],
        scratch=[
            pltpu.VMEM((2, length, lanes), BF16),
            pltpu.VMEM((2, length, lanes), BF16),
            pltpu.VMEM((LANES, length), F32),
            pltpu.VMEM((length, length), F32),
        ],
        flops=10**9,
        scalar=False,
        name="intra",
    )(x_own, g_own, *received, own, rcv)

    def my_heads(v):
        return lax.dynamic_slice(v, (place * half,), (half,))

    skip_row = jnp.broadcast_to(jnp.repeat(my_heads(d_skip), width)[None], (8, lanes))
    rate_row = jnp.broadcast_to(jnp.pad(-jnp.exp(my_heads(a_log)), (0, LANES - half))[None], (8, LANES))
    gx_own, gx_send, pack_own, pack_send, extra = call(
        functools.partial(carry_kernel, heads=heads, width=width, chunks=CHUNKS),
        2 + 5 * CHUNKS + 7,
        [
            ((length, lanes), BF16),
            ((length, lanes), F32),
            ((length, pack), F32),
            ((length, pack), F32),
            ((8, LANES), F32),
        ],
        name="carry",
    )(
        at, x_own, g_own, *received,
        *[v[0] for v in locals_], *[v[1] for v in locals_], *ins, *outs,
        own, rcv, back, grad_bc, rows, skip_row, rate_row,
    )
    pack_rcv = exchange(pack_send)
    gx_rcv = exchange(gx_send)
    cols, extra = call(
        functools.partial(join_kernel, heads=heads), 3, [((length, pack), F32), ((8, LANES), F32)], name="join"
    )(at, pack_own, pack_rcv, extra)
    (grad_x,) = call(merge_kernel, 2, [((length, 2 * lanes), BF16)], name="merge")(at, gx_own, gx_rcv)
    gathered = spread_pieces(cols[None])
    (grad_u,) = call(grad_u_kernel, 4, [((length, model), BF16)], scalar=False, name="grad_u")(
        cols, b_weight, c_weight, tripled
    )
    (blocks,) = call(
        functools.partial(weight_kernel, pieces=len(gathered), heads=heads, state=state),
        2 * len(gathered) + 1,
        [((count, 2 * each + heads, LANES), F32)],
        scalar=False,
        name="weights",
    )(*u_pieces, *gathered, extra)
    mine = jnp.sum(lax.all_to_all(blocks, "seq", 0, 0, tiled=True), axis=0, keepdims=True)
    parts = spread_pieces(mine)
    order = [0]
    for bit in bits:
        order = order + [f ^ bit for f in order]
    rows_out = model // count
    gb, gc, gd, bias, alog, skip = call(
        functools.partial(final_kernel, pieces=len(parts), heads=heads, order=order),
        len(parts),
        [((rows_out, state), F32)] * 2 + [((rows_out, heads), F32)] + [((1, heads), F32)] * 3,
        name="final",
    )(jnp.reshape(group, (1,)).astype(jnp.int32), *parts)
    return grad_x, grad_u, gb, gc, gd, bias[0], alog[0], skip[0]


def solution(mesh):
    rows = P(("dp", "seq"), None)
    in_specs = (rows, rows, rows, P(), P(), P(), P(), P(), P())
    out_specs = (rows, rows, P("seq", None), P("seq", None), P("seq", None), P(), P(), P())
    return jax.shard_map(body, mesh=mesh, in_specs=in_specs, out_specs=out_specs, check_vma=False)
```

time: 511 us -> 179 us (0.35)
  waiting for transfers between devices: 329 us -> 61.6 us
  blocking collectives: 63.7 us -> 0 us
  starting transfers between devices: 0.56 us -> 52.6 us
  matrix products: 30.9 us -> 0 us
  Pallas kernels: 0 us -> 30.7 us
  local copies, waits for them, and re-layouts: 43.2 us -> 18.9 us
  other arithmetic: 27.2 us -> 12.6 us
  between operations: 14.3 us -> 1.25 us
    all_gather x2 -> x0, waiting for transfers between devices: 261 us -> none  [carried_in(): pieces = jax.tree.map(lambda part: lax.all_gather(part, axis), value)]
    ppermute x0 -> x23, starting transfers between devices: none -> 48.2 us  [the longest x4 20.8 us: body(): inward = lax.ppermute(p + decay * inward, 'seq', up)]
    ppermute x0 -> x23, waiting for transfers between devices: none -> 42.1 us  [the longest x5 30.2 us: exchange(): return lax.ppermute(value, 'seq', swap)]
    psum x1 -> x0, blocking collectives: 41.1 us -> none  [body(): small_grads = lax.psum(extras, ('seq', 'dp'))]
    unnamed x5 -> x0, waiting for transfers between devices: 35.9 us -> none
    psum x1 -> x0, waiting for transfers between devices: 32.3 us -> none  [body(): row_grads = lax.psum(row_grads, 'dp')]
    dot_general x18 -> x0, matrix products: 30.9 us -> none  [the longest x1 3.92 us: body(): pair_dots = jnp.einsum('thp,shp->hts', cotangent, inputs, precision=EXACT)]
    pallas_call x0 -> x10, Pallas kernels: none -> 30.7 us  [the longest x1 9.22 us: body(): call(functools.partial(carry_kernel, heads=heads, width=width, chunks=CHU...]
  transfers between devices with their start and end apart: 4 -> 24, of which waited for: 4 -> 7; matrix products, arithmetic and copies ran while one was open for 5% -> 10% of each run, Pallas kernels for 0% -> 14%
where the time goes in v1:
time: 179 us; the launch traced here: 178 us
  waiting for transfers between devices  61.6 us (34%)
  starting transfers between devices  52.6 us (29%)
  Pallas kernels  30.7 us (17%)
  local copies, waits for them, and re-layouts  18.9 us (11%)
  other arithmetic  12.6 us (7%)
    ppermute x5, waiting for transfers between devices, exchange(): return lax.ppermute(value, 'seq', swap)  30.2 us
    ppermute x4, starting transfers between devices, body(): inward = lax.ppermute(p + decay * inward, 'seq', up)  20.8 us
    all_to_all x1, waiting for transfers between devices, body(): lax.all_to_all(blocks, 'seq', 0, 0, tiled=True)  19.5 us
    unnamed x69, local copies, waits for them, and re-layouts  12.4 us
    ppermute x4, waiting for transfers between devices, spread_pieces(): lax.ppermute(sent, 'dp', [(d, d ^ bit) for d in range(groups)])  10.3 us
    pallas_call x1, Pallas kernels, body(): call(functools.partial(carry_kernel, heads=heads, width=width, chunks=CHU...  9.22 us
    pallas_call x1, Pallas kernels, body(): call(functools.partial(intra_kernel, heads=heads, width=width, chunks=CHU...  8.76 us
    ppermute x5, starting transfers between devices, exchange(): return lax.ppermute(value, 'seq', swap)  8.38 us
  transfers between devices with their start and end apart: 24, of which 7 were waited for; matrix products, arithmetic and copies ran while one was open for 10% of the time, Pallas kernels for 14%

profile of v1, /device:TPU:0, one launch (start us, length us, event | category | flops | bytes accessed | tf_op | source)
XLA Modules:
  0.0 177.8 jit_solution(6093587934907745186)
XLA Ops:
  2.7 2.2 %constant_dynamic-slice_fusion = (bf16[128,640]{1,0:T(8,128)(2,1)}, bf16[128,640]{1,0:T(8,128)(2,1)}, bf16[1,128,640]{2,1,0:T(8,128)(2,1)S(1)}, bf16[1,128,640]{...) fusion(bf16[128,2560]{1,0:T(8,128)(2,1)S(1)} %copy-done.26, ...), kind=kLoop, calls=%fused_computation.24 | loop fusion | bytes 2621456 | tf_op jit(solution)/shard_map/slice | solution.py:478
  5.9 1.7 proj.1
  7.6 3.0 %collective-permute-start.1 = (f32[2,128,640]{2,1,0:T(8,128)}, f32[2,128,640]{2,1,0:T(8,128)S(1)}, u32[]{:S(2)}, u32[]{:S(2)}) collective-permute-start(f32[2,128,640]{2,1,0:T(8,128)} %maximum_convert_fusion.1), channel_id=1, source_target_pairs={{0,4},{4,0},{8,12},{12,8},{16,20},{20,16},{24,28},{28,24},{1,5},{5... | collective-permute-start | bytes 1966088 | tf_op jit(solution)/shard_map/ppermute | solution.py:415
  11.5 2.0 %collective-permute-start.2 = (f32[128,384]{1,0:T(8,128)}, f32[128,384]{1,0:T(8,128)}, u32[]{:S(2)}, u32[]{:S(2)}) collective-permute-start(f32[128,384]{1,0:T(8,128)} %get-tuple-element.41), channel_id=1, source_target_pairs={{0,4},{4,0},{8,12},{12,8},{16,20},{20,16},{24,28},{28,24},{1,5},{5... | collective-permute-start | bytes 589832 | tf_op jit(solution)/shard_map/ppermute | solution.py:415
  14.6 2.0 %copy.26 = bf16[4,128,8,80]{1,3,2,0:T(8,128)(2,1)} copy(bf16[4,128,8,80]{1,3,0,2:T(8,128)(2,1)} %bitcast.37) | data formatting | bytes 1310720 | tf_op jit(solution)/shard_map/transpose | solution.py:437
  16.6 27.3 %collective-permute-done.2.pr_ref.refs_3_.refs_11_ = f32[128,384]{1,0:T(8,128)} collective-permute-done((f32[128,384]{1,0:T(8,128)}, f32[128,384]{1,0:T(8,128)}, u32[]{:S(2)}, u32[]{:S(2)}) %collective-permute-start.2) | collective-permute-done | bytes 196640 | tf_op jit(solution)/shard_map/ppermute | solution.py:415
  45.9 2.3 %state.3 = (f32[128,640]{1,0:T(8,128)S(1)}, f32[128,640]{1,0:T(8,128)S(1)}, f32[128,640]{1,0:T(8,128)S(1)}, f32[128,640]{1,0:T(8,128)S(1)}, f32[8,640]{1,0:T(8,128)S(1)}) custom-call(s32[1]{0:T(128)} %bitcast.at_ref, bf16[128,640]{1,0:T(8,128)(2,1)S(1)} %copy-done.13, bf16[128,640]{1,0:T(8,128)(2,1)S(1)} %copy-done.12, ...), custom_call_target="tpu_custom_call" | custom-call | flops 100000000 | bytes 1000000 | tf_op jit(solution)/shard_map/state/pallas_call | solution.py:471
  50.9 5.3 %collective-permute-start.6 = (f32[128,640]{1,0:T(8,128)S(1)}, f32[128,640]{1,0:T(8,128)}, u32[]{:S(2)}, u32[]{:S(2)}) collective-permute-start(f32[128,640]{1,0:T(8,128)S(1)} %get-tuple-element.48), channel_id=1, source_target_pairs={{0,8},{4,12},{8,16},{12,20},{16,24},{20,28},{1,9},{5,13},{9,17},{1... | collective-permute-start | bytes 983048 | tf_op jit(solution)/shard_map/ppermute | solution.py:483
  57.0 1.9 %copy.31 = bf16[2,1,128,640]{3,2,1,0:T(8,128)(2,1)} copy(bf16[2,1,128,640]{2,3,0,1:T(8,128)(2,1)} %constant_dynamic-slice_fusion.6) | data formatting | bytes 655360
  58.9 1.9 %convert_element_type.10 = f32[2,1,128,640]{3,2,1,0:T(8,128)} convert(bf16[2,1,128,640]{3,2,1,0:T(8,128)(2,1)} %copy.31) | non-fusion elementwise | flops 163840 | bytes 983040 | tf_op jit(solution)/shard_map/convert_element_type | solution.py:445
  60.8 1.8 %collective-permute-start.17 = (f32[2,1,128,640]{3,2,1,0:T(8,128)}, f32[2,1,128,640]{3,2,1,0:T(8,128)}, u32[]{:S(2)}, u32[]{:S(2)}) collective-permute-start(f32[2,1,128,640]{3,2,1,0:T(8,128)} %convert_element_type.10), channel_id=1, source_target_pairs={{0,2},{1,3},{2,0},{3,1},{4,6},{5,7},{6,4},{7,5},{8,10},{9,11},{10,... | collective-permute-start | bytes 1966088 | tf_op jit(solution)/shard_map/ppermute | solution.py:447
  64.4 2.2 %state.2 = (f32[128,640]{1,0:T(8,128)S(1)}, f32[128,640]{1,0:T(8,128)S(1)}, f32[128,640]{1,0:T(8,128)S(1)}, f32[128,640]{1,0:T(8,128)S(1)}, f32[8,640]{1,0:T(8,128)S(1)}) custom-call(s32[1]{0:T(128)} %bitcast.at_ref, bf16[128,640]{1,0:T(8,128)(2,1)S(1)} %copy-done.11, bf16[128,640]{1,0:T(8,128)(2,1)S(1)} %copy-done.10, ...), custom_call_target="tpu_custom_call" | custom-call | flops 100000000 | bytes 1000000 | tf_op jit(solution)/shard_map/state/pallas_call | solution.py:471
  66.7 2.8 %collective-permute-start.3 = (f32[128,640]{1,0:T(8,128)S(1)}, f32[128,640]{1,0:T(8,128)S(1)}, u32[]{:S(2)}, u32[]{:S(2)}) collective-permute-start(f32[128,640]{1,0:T(8,128)S(1)} %get-tuple-element.46), channel_id=1, source_target_pairs={{0,8},{4,12},{8,16},{12,20},{16,24},{20,28},{1,9},{5,13},{9,17},{1... | collective-permute-start | bytes 983048 | tf_op jit(solution)/shard_map/ppermute | solution.py:483
  70.8 2.0 %multiply_add_fusion.1 = (f32[128,640]{1,0:T(8,128)}, f32[128,640]{1,0:T(8,128)}) fusion(f32[128,640]{1,0:T(8,128)S(1)} %get-tuple-element.51, f32[128,640]{1,0:T(8,128)} %collective-permute-done.12, f32[640]{0:T(1024)S(1)} %slice_reduce_fusion, f32[128,640]{1,0:T(8,128)S(1)} %get-tuple-element.48, f32[128,640]{1,0:T(8,128)} %collective-permute-done.6), kind=kLoop, calls=%fused_computation.12 | loop fusion | flops 327680 | bytes 1968640 | tf_op jit(solution)/shard_map/add | solution.py:487
  74.2 6.2 %collective-permute-start.7 = (f32[128,640]{1,0:T(8,128)}, f32[128,640]{1,0:T(8,128)}, u32[]{:S(2)}, u32[]{:S(2)}) collective-permute-start(f32[128,640]{1,0:T(8,128)} %get-tuple-element.99), channel_id=1, source_target_pairs={{0,8},{4,12},{8,16},{12,20},{16,24},{20,28},{1,9},{5,13},{9,17},{1... | collective-permute-start | bytes 983048 | tf_op jit(solution)/shard_map/ppermute | solution.py:486
  80.4 1.6 collective-permute-done.9
  84.3 5.3 %collective-permute-start.4 = (f32[128,640]{1,0:T(8,128)}, f32[128,640]{1,0:T(8,128)}, u32[]{:S(2)}, u32[]{:S(2)}) collective-permute-start(f32[128,640]{1,0:T(8,128)} %get-tuple-element.103), channel_id=1, source_target_pairs={{0,8},{4,12},{8,16},{12,20},{16,24},{20,28},{1,9},{5,13},{9,17},{1... | collective-permute-start | bytes 983048 | tf_op jit(solution)/shard_map/ppermute | solution.py:486
  91.2 1.4 collective-permute-start.14
  92.6 4.6 %collective-permute-start.8 = (f32[128,640]{1,0:T(8,128)S(1)}, f32[128,640]{1,0:T(8,128)S(1)}, u32[]{:S(2)}, u32[]{:S(2)}) collective-permute-start(f32[128,640]{1,0:T(8,128)S(1)} %get-tuple-element.97), channel_id=1, source_target_pairs={{0,8},{4,12},{8,16},{12,20},{16,24},{20,28},{1,9},{5,13},{9,17},{1... | collective-permute-start | bytes 983048 | tf_op jit(solution)/shard_map/ppermute | solution.py:486
  99.6 4.7 %collective-permute-start.5 = (f32[128,640]{1,0:T(8,128)S(1)}, f32[128,640]{1,0:T(8,128)S(1)}, u32[]{:S(2)}, u32[]{:S(2)}) collective-permute-start(f32[128,640]{1,0:T(8,128)S(1)} %get-tuple-element.101), channel_id=1, source_target_pairs={{0,8},{4,12},{8,16},{12,20},{16,24},{20,28},{1,9},{5,13},{9,17},{1... | collective-permute-start | bytes 983048 | tf_op jit(solution)/shard_map/ppermute | solution.py:486
  104.5 8.8 %intra.1 = (f32[2,128,1280]{2,1,0:T(8,128)S(1)}, f32[2,128,256]{2,1,0:T(8,128)S(1)}, f32[2,128,128]{2,1,0:T(8,128)S(1)}) custom-call(bf16[128,1280]{1,0:T(8,128)(2,1)S(1)} %get-tuple-element.109.xo_ref, bf16[128,1280]{1,0:T(8,128)(2,1)S(1)} %get-tuple-element.108.go_ref, f32[2,128,640]{2,1,0:T(8,128)S(1)} %collective-permute-done.xgr_ref.refs_0_, ...), custom_call_target="tpu_custom_call" | custom-call | flops 1000000000 | bytes 1000000 | tf_op jit(solution)/shard_map/intra/pallas_call | solution.py:490
  114.5 9.2 %carry.1 = (bf16[128,1280]{1,0:T(8,128)(2,1)S(1)}, f32[128,1280]{1,0:T(8,128)}, f32[128,384]{1,0:T(8,128)S(1)}, f32[128,384]{1,0:T(8,128)S(1)}, f32[8,128]{1,0:T(8,128)S(1)}) custom-call(s32[1]{0:T(128)} %bitcast.at_ref, bf16[128,1280]{1,0:T(8,128)(2,1)S(1)} %get-tuple-element.109.xo_ref, bf16[128,1280]{1,0:T(8,128)(2,1)S(1)} %get-tuple-element.108.go_ref, ...), custom_call_target="tpu_custom_call" | custom-call | flops 100000000 | bytes 1000000 | tf_op jit(solution)/shard_map/carry/pallas_call | solution.py:510
  124.5 1.5 collective-permute-start.16
  127.3 2.8 %collective-permute-done.16.rcv_ref = f32[128,384]{1,0:T(8,128)S(1)} collective-permute-done((f32[128,384]{1,0:T(8,128)S(1)}, f32[128,384]{1,0:T(8,128)S(1)}, u32[]{:S(2)}, u32[]{:S(2)}) %collective-permute-start.16) | collective-permute-done | bytes 196640 | tf_op jit(solution)/shard_map/ppermute | solution.py:415
  131.7 4.3 %collective-permute-done.19.refs_4_ = f32[1,128,384]{2,1,0:T(8,128)S(1)} collective-permute-done((f32[1,128,384]{2,1,0:T(8,128)S(1)}, f32[1,128,384]{2,1,0:T(8,128)S(1)}, u32[]{:S(2)}, u32[]{:S(2)}) %collective-permute-start.19) | collective-permute-done | bytes 196640 | tf_op jit(solution)/shard_map/ppermute | solution.py:433
  136.9 1.9 %collective-permute-done.20.refs_5_ = f32[2,128,384]{2,1,0:T(8,128)} collective-permute-done((f32[2,128,384]{2,1,0:T(8,128)}, f32[2,128,384]{2,1,0:T(8,128)}, u32[]{:S(2)}, u32[]{:S(2)}) %collective-permute-start.20) | collective-permute-done | bytes 393248 | tf_op jit(solution)/shard_map/ppermute | solution.py:433
  138.8 2.7 %weights.1 = f32[8,200,128]{2,1,0:T(8,128)} custom-call(bf16[1,128,640]{2,1,0:T(8,128)(2,1)S(1)} %bitcast.34, f32[1,128,640]{2,1,0:T(8,128)S(1)} %get-tuple-element.87.refs_1_, f32[2,128,640]{2,1,0:T(8,128)S(1)} %bitcast.33, f32[1,128,384]{2,1,0:T(8,128)S(1)} %bitcast.29, f32[1,128,384]{2,1,0:T(8,128)S(1)} %collective-permute-done.19.refs_4_, ...), custom_call_target="tpu_custom_call" | custom-call | flops 100000000 | bytes 1000000 | tf_op jit(solution)/shard_map/weights/pallas_call | solution.py:536
  141.5 4.3 %all-to-all-start = ((f32[8,200,128]{2,1,0:T(8,128)}), f32[8,200,128]{2,1,0:T(8,128)}, u32[]{:S(2)}, u32[]{:S(2)}) async-start(f32[8,200,128]{2,1,0:T(8,128)} %weights.1), calls=%async_computation | async-start | bytes 1638400 | tf_op jit(solution)/shard_map/all_to_all | solution.py:543
  145.9 1.9 %collective-permute-start.15 = (f32[128,1280]{1,0:T(8,128)}, f32[128,1280]{1,0:T(8,128)S(1)}, u32[]{:S(2)}, u32[]{:S(2)}) collective-permute-start(f32[128,1280]{1,0:T(8,128)} %get-tuple-element.56), channel_id=1, source_target_pairs={{0,4},{4,0},{8,12},{12,8},{16,20},{20,16},{24,28},{28,24},{1,5},{5... | collective-permute-start | bytes 1966088 | tf_op jit(solution)/shard_map/ppermute | solution.py:415
  147.8 19.5 %all-to-all-done = f32[8,200,128]{2,1,0:T(8,128)} async-done(((f32[8,200,128]{2,1,0:T(8,128)}), f32[8,200,128]{2,1,0:T(8,128)}, u32[]{:S(2)}, u32[]{:S(2)}) %all-to-all-start) | async-done | bytes 819232 | tf_op jit(solution)/shard_map/all_to_all | solution.py:543
  169.1 4.2 %collective-permute-done.21.refs_1_ = f32[1,200,128]{2,1,0:T(8,128)S(1)} collective-permute-done((f32[1,200,128]{2,1,0:T(8,128)S(1)}, f32[1,200,128]{2,1,0:T(8,128)S(1)}, u32[]{:S(2)}, u32[]{:S(2)}) %collective-permute-start.21) | collective-permute-done | bytes 102432 | tf_op jit(solution)/shard_map/ppermute | solution.py:433
  173.4 2.0 %grad_u.1 = bf16[128,2560]{1,0:T(8,128)(2,1)} custom-call(f32[128,384]{1,0:T(8,128)S(1)} %get-tuple-element.60.cols_ref, bf16[2560,128]{1,0:T(8,128)(2,1)S(1)} %copy-done.2, bf16[2560,128]{1,0:T(8,128)(2,1)S(1)} %copy-done.4, bf16[2560,128]{1,0:T(8,128)(2,1)S(1)} %fusion.4.wd_ref), custom_call_target="tpu_custom_call" | custom-call | flops 100000000 | bytes 1000000 | tf_op jit(solution)/shard_map/grad_u/pallas_call | solution.py:533
  (125 shorter events, 31.2 us)
Async XLA Ops:
  7.6 36.3 %collective-permute-start.1 = (f32[2,128,640]{2,1,0:T(8,128)}, f32[2,128,640]{2,1,0:T(8,128)S(1)}, u32[]{:S(2)}, u32[]{:S(2)}) collective-permute-start(f32[2,128,640]{2,1,0:T(8,128)} %maximum_convert_fusion.1), channel_id=1, source_target_pairs={{0,4},{4,0},{8,12},{12,8},{16,20},{20,16},{24,28},{28,24},{1,5},{5... | collective-permute-start | bytes 1966088 | tf_op jit(solution)/shard_map/ppermute | solution.py:415
  11.5 51.1 %collective-permute-start = (f32[2,128,640]{2,1,0:T(8,128)}, f32[2,128,640]{2,1,0:T(8,128)S(1)}, u32[]{:S(2)}, u32[]{:S(2)}) collective-permute-start(f32[2,128,640]{2,1,0:T(8,128)} %maximum_convert_fusion), channel_id=1, source_target_pairs={{0,4},{4,0},{8,12},{12,8},{16,20},{20,16},{24,28},{28,24},{1,5},{5... | collective-permute-start | bytes 1966088 | tf_op jit(solution)/shard_map/ppermute | solution.py:415
  11.5 32.4 %collective-permute-start.2 = (f32[128,384]{1,0:T(8,128)}, f32[128,384]{1,0:T(8,128)}, u32[]{:S(2)}, u32[]{:S(2)}) collective-permute-start(f32[128,384]{1,0:T(8,128)} %get-tuple-element.41), channel_id=1, source_target_pairs={{0,4},{4,0},{8,12},{12,8},{16,20},{20,16},{24,28},{28,24},{1,5},{5... | collective-permute-start | bytes 589832 | tf_op jit(solution)/shard_map/ppermute | solution.py:415
  43.9 60.6 %copy-start = (f32[2,128,640]{2,1,0:T(8,128)}, f32[2,128,640]{2,1,0:T(8,128)S(1)}, u32[]{:S(2)}) copy-start(f32[2,128,640]{2,1,0:T(8,128)S(1)} %collective-permute-done.1.xgr_ref.refs_1_) | copy-start | bytes 1966084
  49.7 21.1 %collective-permute-start.12 = (f32[128,640]{1,0:T(8,128)S(1)}, f32[128,640]{1,0:T(8,128)}, u32[]{:S(2)}, u32[]{:S(2)}) collective-permute-start(f32[128,640]{1,0:T(8,128)S(1)} %get-tuple-element.51), channel_id=1, source_target_pairs={{8,0},{12,4},{16,8},{20,12},{24,16},{28,20},{9,1},{13,5},{17,9},{2... | collective-permute-start | bytes 983048 | tf_op jit(solution)/shard_map/ppermute | solution.py:484
  50.9 19.8 %collective-permute-start.6 = (f32[128,640]{1,0:T(8,128)S(1)}, f32[128,640]{1,0:T(8,128)}, u32[]{:S(2)}, u32[]{:S(2)}) collective-permute-start(f32[128,640]{1,0:T(8,128)S(1)} %get-tuple-element.48), channel_id=1, source_target_pairs={{0,8},{4,12},{8,16},{12,20},{16,24},{20,28},{1,9},{5,13},{9,17},{1... | collective-permute-start | bytes 983048 | tf_op jit(solution)/shard_map/ppermute | solution.py:483
  60.8 65.4 %collective-permute-start.17 = (f32[2,1,128,640]{3,2,1,0:T(8,128)}, f32[2,1,128,640]{3,2,1,0:T(8,128)}, u32[]{:S(2)}, u32[]{:S(2)}) collective-permute-start(f32[2,1,128,640]{3,2,1,0:T(8,128)} %convert_element_type.10), channel_id=1, source_target_pairs={{0,2},{1,3},{2,0},{3,1},{4,6},{5,7},{6,4},{7,5},{8,10},{9,11},{10,... | collective-permute-start | bytes 1966088 | tf_op jit(solution)/shard_map/ppermute | solution.py:447
  66.6 16.3 %copy-start.6 = (f32[128,640]{1,0:T(8,128)}, f32[128,640]{1,0:T(8,128)S(1)}, u32[]{:S(2)}) copy-start(f32[128,640]{1,0:T(8,128)S(1)} %get-tuple-element.46) | copy-start | bytes 983044
  66.6 16.3 %copy-start.8 = (f32[128,640]{1,0:T(8,128)}, f32[128,640]{1,0:T(8,128)S(1)}, u32[]{:S(2)}) copy-start(f32[128,640]{1,0:T(8,128)S(1)} %get-tuple-element.50) | copy-start | bytes 983044
  66.7 16.3 %copy-start.18 = (f32[128,640]{1,0:T(8,128)}, f32[128,640]{1,0:T(8,128)S(1)}, u32[]{:S(2)}) copy-start(f32[128,640]{1,0:T(8,128)S(1)} %get-tuple-element.42.refs_2_) | copy-start | bytes 983044
  66.7 16.3 %copy-start.20 = (f32[128,640]{1,0:T(8,128)}, f32[128,640]{1,0:T(8,128)S(1)}, u32[]{:S(2)}) copy-start(f32[128,640]{1,0:T(8,128)S(1)} %get-tuple-element.44.refs_4_) | copy-start | bytes 983044
  66.7 13.7 %collective-permute-start.3 = (f32[128,640]{1,0:T(8,128)S(1)}, f32[128,640]{1,0:T(8,128)S(1)}, u32[]{:S(2)}, u32[]{:S(2)}) collective-permute-start(f32[128,640]{1,0:T(8,128)S(1)} %get-tuple-element.46), channel_id=1, source_target_pairs={{0,8},{4,12},{8,16},{12,20},{16,24},{20,28},{1,9},{5,13},{9,17},{1... | collective-permute-start | bytes 983048 | tf_op jit(solution)/shard_map/ppermute | solution.py:483
  69.4 12.6 %collective-permute-start.9 = (f32[128,640]{1,0:T(8,128)S(1)}, f32[128,640]{1,0:T(8,128)S(1)}, u32[]{:S(2)}, u32[]{:S(2)}) collective-permute-start(f32[128,640]{1,0:T(8,128)S(1)} %get-tuple-element.50), channel_id=1, source_target_pairs={{8,0},{12,4},{16,8},{20,12},{24,16},{28,20},{9,1},{13,5},{17,9},{2... | collective-permute-start | bytes 983048 | tf_op jit(solution)/shard_map/ppermute | solution.py:484
  72.8 16.8 %copy-start.31 = (f32[40]{0:T(128)S(1)}, f32[40]{0:T(128)}, u32[]{:S(2)}) copy-start(f32[40]{0:T(128)} %param.17) | copy-start | bytes 484
  72.8 17.1 %collective-permute-start.13 = (f32[128,640]{1,0:T(8,128)}, f32[128,640]{1,0:T(8,128)}, u32[]{:S(2)}, u32[]{:S(2)}) collective-permute-start(f32[128,640]{1,0:T(8,128)} %get-tuple-element.98), channel_id=1, source_target_pairs={{8,0},{12,4},{16,8},{20,12},{24,16},{28,20},{9,1},{13,5},{17,9},{2... | collective-permute-start | bytes 983048 | tf_op jit(solution)/shard_map/ppermute | solution.py:487
  74.2 15.7 %collective-permute-start.7 = (f32[128,640]{1,0:T(8,128)}, f32[128,640]{1,0:T(8,128)}, u32[]{:S(2)}, u32[]{:S(2)}) collective-permute-start(f32[128,640]{1,0:T(8,128)} %get-tuple-element.99), channel_id=1, source_target_pairs={{0,8},{4,12},{8,16},{12,20},{16,24},{20,28},{1,9},{5,13},{9,17},{1... | collective-permute-start | bytes 983048 | tf_op jit(solution)/shard_map/ppermute | solution.py:486
  83.0 14.2 %collective-permute-start.10 = (f32[128,640]{1,0:T(8,128)}, f32[128,640]{1,0:T(8,128)}, u32[]{:S(2)}, u32[]{:S(2)}) collective-permute-start(f32[128,640]{1,0:T(8,128)} %get-tuple-element.102), channel_id=1, source_target_pairs={{8,0},{12,4},{16,8},{20,12},{24,16},{28,20},{9,1},{13,5},{17,9},{2... | collective-permute-start | bytes 983048 | tf_op jit(solution)/shard_map/ppermute | solution.py:487
  84.3 12.9 %collective-permute-start.4 = (f32[128,640]{1,0:T(8,128)}, f32[128,640]{1,0:T(8,128)}, u32[]{:S(2)}, u32[]{:S(2)}) collective-permute-start(f32[128,640]{1,0:T(8,128)} %get-tuple-element.103), channel_id=1, source_target_pairs={{0,8},{4,12},{8,16},{12,20},{16,24},{20,28},{1,9},{5,13},{9,17},{1... | collective-permute-start | bytes 983048 | tf_op jit(solution)/shard_map/ppermute | solution.py:486
  91.1 13.3 %copy-start.27 = (bf16[128,2560]{1,0:T(8,128)(2,1)S(1)}, bf16[128,2560]{1,0:T(8,128)(2,1)}, u32[]{:S(2)}) copy-start(bf16[128,2560]{1,0:T(8,128)(2,1)} %param.11) | copy-start | bytes 1966084
  91.2 23.2 %collective-permute-start.14 = (f32[128,640]{1,0:T(8,128)S(1)}, f32[128,640]{1,0:T(8,128)S(1)}, u32[]{:S(2)}, u32[]{:S(2)}) collective-permute-start(f32[128,640]{1,0:T(8,128)S(1)} %get-tuple-element.96), channel_id=1, source_target_pairs={{8,0},{12,4},{16,8},{20,12},{24,16},{28,20},{9,1},{13,5},{17,9},{2... | collective-permute-start | bytes 983048 | tf_op jit(solution)/shard_map/ppermute | solution.py:487
  92.6 21.8 %collective-permute-start.8 = (f32[128,640]{1,0:T(8,128)S(1)}, f32[128,640]{1,0:T(8,128)S(1)}, u32[]{:S(2)}, u32[]{:S(2)}) collective-permute-start(f32[128,640]{1,0:T(8,128)S(1)} %get-tuple-element.97), channel_id=1, source_target_pairs={{0,8},{4,12},{8,16},{12,20},{16,24},{20,28},{1,9},{5,13},{9,17},{1... | collective-permute-start | bytes 983048 | tf_op jit(solution)/shard_map/ppermute | solution.py:486
  98.3 16.1 %collective-permute-start.11 = (f32[128,640]{1,0:T(8,128)S(1)}, f32[128,640]{1,0:T(8,128)S(1)}, u32[]{:S(2)}, u32[]{:S(2)}) collective-permute-start(f32[128,640]{1,0:T(8,128)S(1)} %get-tuple-element.100), channel_id=1, source_target_pairs={{8,0},{12,4},{16,8},{20,12},{24,16},{28,20},{9,1},{13,5},{17,9},{2... | collective-permute-start | bytes 983048 | tf_op jit(solution)/shard_map/ppermute | solution.py:487
  99.6 14.8 %collective-permute-start.5 = (f32[128,640]{1,0:T(8,128)S(1)}, f32[128,640]{1,0:T(8,128)S(1)}, u32[]{:S(2)}, u32[]{:S(2)}) collective-permute-start(f32[128,640]{1,0:T(8,128)S(1)} %get-tuple-element.101), channel_id=1, source_target_pairs={{0,8},{4,12},{8,16},{12,20},{16,24},{20,28},{1,9},{5,13},{9,17},{1... | collective-permute-start | bytes 983048 | tf_op jit(solution)/shard_map/ppermute | solution.py:486
  124.5 5.7 %collective-permute-start.16 = (f32[128,384]{1,0:T(8,128)S(1)}, f32[128,384]{1,0:T(8,128)S(1)}, u32[]{:S(2)}, u32[]{:S(2)}) collective-permute-start(f32[128,384]{1,0:T(8,128)S(1)} %get-tuple-element.58), channel_id=1, source_target_pairs={{0,4},{4,0},{8,12},{12,8},{16,20},{20,16},{24,28},{28,24},{1,5},{5... | collective-permute-start | bytes 589832 | tf_op jit(solution)/shard_map/ppermute | solution.py:415
  130.2 5.7 %collective-permute-start.19 = (f32[1,128,384]{2,1,0:T(8,128)S(1)}, f32[1,128,384]{2,1,0:T(8,128)S(1)}, u32[]{:S(2)}, u32[]{:S(2)}) collective-permute-start(f32[1,128,384]{2,1,0:T(8,128)S(1)} %bitcast.27), channel_id=1, source_target_pairs={{0,2},{1,3},{2,0},{3,1},{4,6},{5,7},{6,4},{7,5},{8,10},{9,11},{10,... | collective-permute-start | bytes 589832 | tf_op jit(solution)/shard_map/ppermute | solution.py:433
  131.7 5.2 %collective-permute-start.18 = (f32[1,2,128,640]{3,2,1,0:T(8,128)}, f32[1,2,128,640]{3,2,1,0:T(8,128)S(1)}, u32[]{:S(2)}, u32[]{:S(2)}) collective-permute-start(f32[1,2,128,640]{3,2,1,0:T(8,128)} %pad_maximum_fusion), channel_id=1, source_target_pairs={{0,1},{1,0},{2,3},{3,2},{4,5},{5,4},{6,7},{7,6},{8,9},{9,8},{10,11... | collective-permute-start | bytes 1966088 | tf_op jit(solution)/shard_map/ppermute | solution.py:447
  136.7 2.1 %collective-permute-start.20 = (f32[2,128,384]{2,1,0:T(8,128)}, f32[2,128,384]{2,1,0:T(8,128)}, u32[]{:S(2)}, u32[]{:S(2)}) collective-permute-start(f32[2,128,384]{2,1,0:T(8,128)} %pad_maximum_fusion.1), channel_id=1, source_target_pairs={{0,1},{1,0},{2,3},{3,2},{4,5},{5,4},{6,7},{7,6},{8,9},{9,8},{10,11... | collective-permute-start | bytes 1179656 | tf_op jit(solution)/shard_map/ppermute | solution.py:433
  141.5 31.8 %copy-start.4 = (bf16[2560,128]{1,0:T(8,128)(2,1)S(1)}, bf16[2560,128]{1,0:T(8,128)(2,1)}, u32[]{:S(2)}) copy-start(bf16[2560,128]{1,0:T(8,128)(2,1)} %wc_ref.3) | copy-start | bytes 1966084
  141.5 25.8 %all-to-all-start = ((f32[8,200,128]{2,1,0:T(8,128)}), f32[8,200,128]{2,1,0:T(8,128)}, u32[]{:S(2)}, u32[]{:S(2)}) async-start(f32[8,200,128]{2,1,0:T(8,128)} %weights.1), calls=%async_computation | async-start | bytes 1638400 | tf_op jit(solution)/shard_map/all_to_all | solution.py:543
  145.9 29.5 %collective-permute-start.15 = (f32[128,1280]{1,0:T(8,128)}, f32[128,1280]{1,0:T(8,128)S(1)}, u32[]{:S(2)}, u32[]{:S(2)}) collective-permute-start(f32[128,1280]{1,0:T(8,128)} %get-tuple-element.56), channel_id=1, source_target_pairs={{0,4},{4,0},{8,12},{12,8},{16,20},{20,16},{24,28},{28,24},{1,5},{5... | collective-permute-start | bytes 1966088 | tf_op jit(solution)/shard_map/ppermute | solution.py:415
  168.5 4.7 %collective-permute-start.21 = (f32[1,200,128]{2,1,0:T(8,128)S(1)}, f32[1,200,128]{2,1,0:T(8,128)S(1)}, u32[]{:S(2)}, u32[]{:S(2)}) collective-permute-start(f32[1,200,128]{2,1,0:T(8,128)S(1)} %bitcast.30), channel_id=1, source_target_pairs={{0,2},{1,3},{2,0},{3,1},{4,6},{5,7},{6,4},{7,5},{8,10},{9,11},{10,... | collective-permute-start | bytes 307208 | tf_op jit(solution)/shard_map/ppermute | solution.py:433
  173.3 3.0 %collective-permute-start.22 = (f32[2,200,128]{2,1,0:T(8,128)S(1)}, f32[2,200,128]{2,1,0:T(8,128)S(1)}, u32[]{:S(2)}, u32[]{:S(2)}) collective-permute-start(f32[2,200,128]{2,1,0:T(8,128)S(1)} %pad_maximum_fusion.2), channel_id=1, source_target_pairs={{0,1},{1,0},{2,3},{3,2},{4,5},{5,4},{6,7},{7,6},{8,9},{9,8},{10,11... | collective-permute-start | bytes 614408 | tf_op jit(solution)/shard_map/ppermute | solution.py:433
  (24 other events, 116.7 us)
